TPU v7x, 32 devices: a whole 2x2x4 slice. The times are simulated.
32 devices in a mesh: gx: 2 (over y), gy: 4 (over x, core), gz: 4 (over z).
Axes of the slice: x: 2, y: 2, z: 4, core: 2. Of those that a mesh axis runs over, the one named last changes fastest.
Arguments:
- loads: float32 [16, 4, 16, 1024], P(None, 'gx', 'gy', 'gz'), may hold values from -60 to 60
- moduli: float32 [8], replicated, may hold values from 0.5 to 4
- material: int32 [4, 16, 1024], P('gx', 'gy', 'gz'), may hold values from 0 to 7
Outputs:
- solution: float32 [16, 4, 16, 1024], P(None, 'gx', 'gy', 'gz')
- residual: float32 [16, 4, 16, 1024], P(None, 'gx', 'gy', 'gz')
All inputs are finite; a program needn't handle non-finite values.
Results may differ from a plain program's by a relative error of at most 0.005.
The roundings to bfloat16 on the way count: a program that leaves them out, or rounds other values in their place, can miss the bound.
Values may be sent and summed in bfloat16 or wider, within the bound.
A program may use at most 64 MiB of HBM per device.

v0:
```python
import jax
import jax.numpy as jnp
import numpy as np
from jax import lax
from jax.sharding import PartitionSpec as P

ITERS = 2
SIGMA = 0.25


def padded_2(cells, sides, width):
    for axis, dim in sides:
        count = lax.axis_size(axis)
        ends = count - 1
        head = lax.slice_in_dim(cells, 0, width, axis=dim)
        tail = lax.slice_in_dim(cells, cells.shape[dim] - width, cells.shape[dim], axis=dim)
        cells = jnp.concatenate(
            [
                lax.ppermute(tail, axis, [(i, (i + 1) % count) for i in range(ends)]),
                cells,
                lax.ppermute(head, axis, [((i + 1) % count, i) for i in range(ends)]),
            ],
            axis=dim,
        )
    return cells


def stiffness_table():
    line_mass = np.array([[1.0 / 3.0, 1.0 / 6.0], [1.0 / 6.0, 1.0 / 3.0]])
    line_stiff = np.array([[1.0, -1.0], [-1.0, 1.0]])
    table = np.zeros((8, 8))
    for target in range(8):
        for source in range(8):
            target_bits = [target >> 2 & 1, target >> 1 & 1, target & 1]
            source_bits = [source >> 2 & 1, source >> 1 & 1, source & 1]
            total = 0.0
            for stiff_dim in range(3):
                factor = 1.0
                for other in range(3):
                    if other == stiff_dim:
                        factor = factor * line_stiff[target_bits[other], source_bits[other]]
                    else:
                        factor = factor * line_mass[target_bits[other], source_bits[other]]
                total = total + factor
            table[target, source] = total
    return table


def corner_bits(corner):
    return (corner >> 2 & 1, corner >> 1 & 1, corner & 1)


def apply_operator(field, weights, kernel):
    lowered = field.astype(jnp.bfloat16)
    padded = padded_2(lowered, (("gx", 1), ("gy", 2), ("gz", 3)), 1)
    size_x, size_y, size_z = (field.shape[1], field.shape[2], field.shape[3])
    pieces = []
    for corner in range(8):
        bit_x, bit_y, bit_z = corner_bits(corner)
        pieces.append(
            padded[
                :,
                bit_x : bit_x + size_x + 1,
                bit_y : bit_y + size_y + 1,
                bit_z : bit_z + size_z + 1,
            ]
        )
    stacked = jnp.stack(pieces)
    total = SIGMA * field
    for corner in range(8):
        bit_x, bit_y, bit_z = corner_bits(corner)
        part = (
            jnp.einsum("b,bcxyz->cxyz", kernel[corner], stacked, preferred_element_type=jnp.float32)
            * weights
        )
        total = (
            total
            + part[
                :,
                1 - bit_x : 1 - bit_x + size_x,
                1 - bit_y : 1 - bit_y + size_y,
                1 - bit_z : 1 - bit_z + size_z,
            ]
        )
    return total


def local_gram(left, right):
    return jnp.einsum("cxyz,dxyz->cd", left, right, precision=lax.Precision.HIGHEST)


def combine(block, coeffs):
    return jnp.einsum("cxyz,cd->dxyz", block, coeffs, precision=lax.Precision.HIGHEST)


def solve_small(matrix, rhs_small):
    factor = jnp.linalg.cholesky(matrix)
    return jax.scipy.linalg.cho_solve((factor, True), rhs_small)


def residual_gram(residual):
    return lax.psum(local_gram(residual, residual), ("gx", "gy", "gz"))


def on_device(loads, moduli, material):
    kernel = jnp.asarray(stiffness_table(), jnp.float32).astype(jnp.bfloat16)
    levels = jnp.arange(moduli.shape[0], dtype=jnp.int32)
    node_modulus = jnp.sum(jnp.where(material[..., None] == levels, moduli, 0.0), axis=-1)
    padded_mod = padded_2(node_modulus, (("gx", 0), ("gy", 1), ("gz", 2)), 1)
    size_x, size_y, size_z = material.shape
    weights = jnp.zeros((size_x + 1, size_y + 1, size_z + 1), jnp.float32)
    for corner in range(8):
        bit_x, bit_y, bit_z = corner_bits(corner)
        weights = (
            weights
            + padded_mod[
                bit_x : bit_x + size_x + 1, bit_y : bit_y + size_y + 1, bit_z : bit_z + size_z + 1
            ]
        )
    weights = weights * 0.125
    solution = jnp.zeros_like(loads)
    residual = loads
    direction = loads
    current = residual_gram(residual)
    for iteration in range(ITERS):
        image = apply_operator(direction, weights, kernel)
        curvature, cross, image_sq = lax.psum(
            (local_gram(direction, image), local_gram(image, residual), local_gram(image, image)),
            ("gx", "gy", "gz"),
        )
        alpha = solve_small(curvature, current)
        solution = solution + combine(direction, alpha)
        residual = residual - combine(image, alpha)
        if iteration + 1 < ITERS:
            high = lax.Precision.HIGHEST
            cross_term = jnp.dot(alpha.T, cross, precision=high)
            quad_term = jnp.dot(jnp.dot(alpha.T, image_sq, precision=high), alpha, precision=high)
            updated = current - cross_term - cross_term.T + quad_term
            beta = solve_small(current, updated)
            direction = residual + combine(direction, beta)
            current = updated
    return (solution, residual)


def solution(mesh):
    in_specs = (P(None, "gx", "gy", "gz"), P(), P("gx", "gy", "gz"))
    out_specs = (P(None, "gx", "gy", "gz"), P(None, "gx", "gy", "gz"))
    return jax.shard_map(
        on_device, mesh=mesh, in_specs=in_specs, out_specs=out_specs, check_vma=False
    )
```

profile of v0, /device:TPU:0, one launch (start us, length us, event | category | flops | bytes accessed | tf_op | source)
XLA Modules:
  0.0 185.7 jit_solution(12359744168205889732)
XLA Ops:
  0.6 0.8 select_reduce_fusion
  1.4 4.9 %collective-permute-start.6 = (f32[1,4,256]{2,1,0:T(4,128)S(1)}, f32[1,4,256]{2,1,0:T(4,128)S(1)}, u32[]{:S(2)}, u32[]{:S(2)}) collective-permute-start(f32[1,4,256]{2,1,0:T(4,128)S(1)} %get-tuple-element.42), channel_id=1, source_target_pairs={{0,16},{1,17},{2,18},{3,19},{4,20},{5,21},{6,22},{7,23},{8,24},{9,... | collective-permute-start | bytes 12296 | tf_op jit(solution)/shard_map/ppermute | solution.py:19
  6.4 1.3 collective-permute-start.7
  7.7 0.9 convert_element_type.9
  8.6 4.5 %collective-permute-start = (bf16[16,1,4,256]{3,2,1,0:T(4,128)(2,1)S(1)}, bf16[16,1,4,256]{3,2,1,0:T(4,128)(2,1)S(1)}, u32[]{:S(2)}, u32[]{:S(2)}) collective-permute-start(bf16[16,1,4,256]{3,2,1,0:T(4,128)(2,1)S(1)} %get-tuple-element.26), channel_id=1, source_target_pairs={{0,16},{1,17},{2,18},{3,19},{4,20},{5,21},{6,22},{7,23},{8,24},{9,... | collective-permute-start | bytes 98312 | tf_op jit(solution)/shard_map/ppermute | solution.py:19
  13.2 1.3 collective-permute-start.1
  14.5 1.3 collective-permute-start.8
  15.8 1.3 collective-permute-start.9
  17.1 1.3 convolution_bitcast_fusion.4
  18.4 2.2 %collective-permute-done.9 = f32[4,1,256]{2,1,0:T(1,128)S(1)} collective-permute-done((f32[4,1,256]{2,1,0:T(1,128)S(1)}, f32[4,1,256]{2,1,0:T(1,128)S(1)}, u32[]{:S(2)}, u32[]{:S(2)}) %collective-permute-start.9) | collective-permute-done | bytes 4128 | tf_op jit(solution)/shard_map/ppermute | solution.py:21
  20.7 3.5 %collective-permute-start.10 = (f32[4,6,1]{2,1,0:T(8,128)S(1)}, f32[4,6,1]{2,1,0:T(8,128)S(1)}, u32[]{:S(2)}, u32[]{:S(2)}) collective-permute-start(f32[4,6,1]{2,1,0:T(8,128)S(1)} %get-tuple-element.36), channel_id=1, source_target_pairs={{0,1},{1,2},{2,3},{4,5},{5,6},{6,7},{8,9},{9,10},{10,11},{12,13},{... | collective-permute-start | bytes 296 | tf_op jit(solution)/shard_map/ppermute | solution.py:19
  24.2 1.3 collective-permute-start.11
  25.6 4.2 %collective-permute-done.11 = f32[4,6,1]{2,1,0:T(8,128)S(1)} collective-permute-done((f32[4,6,1]{2,1,0:T(8,128)S(1)}, f32[4,6,1]{2,1,0:T(8,128)S(1)}, u32[]{:S(2)}, u32[]{:S(2)}) %collective-permute-start.11) | collective-permute-done | bytes 128 | tf_op jit(solution)/shard_map/ppermute | solution.py:21
  30.1 2.8 %collective-permute-start.2 = (bf16[16,4,1,256]{3,2,1,0:T(2,128)(2,1)S(1)}, bf16[16,4,1,256]{3,2,1,0:T(2,128)(2,1)S(1)}, u32[]{:S(2)}, u32[]{:S(2)}) collective-permute-start(bf16[16,4,1,256]{3,2,1,0:T(2,128)(2,1)S(1)} %get-tuple-element.22), channel_id=1, source_target_pairs={{0,4},{4,8},{8,12},{1,5},{5,9},{9,13},{2,6},{6,10},{10,14},{3,7},{... | collective-permute-start | bytes 98312 | tf_op jit(solution)/shard_map/ppermute | solution.py:19
  33.0 1.3 collective-permute-start.3
  34.3 2.8 %collective-permute-done.3 = bf16[16,4,1,256]{3,2,1,0:T(2,128)(2,1)S(1)} collective-permute-done((bf16[16,4,1,256]{3,2,1,0:T(2,128)(2,1)S(1)}, bf16[16,4,1,256]{3,2,1,0:T(2,128)(2,1)S(1)}, u32[]{:S(2)}, u32[]{:S(2)}) %collective-permute-start.3) | collective-permute-done | bytes 32800 | tf_op jit(solution)/shard_map/ppermute | solution.py:21
  37.5 3.5 %collective-permute-start.4 = (bf16[16,4,6,1]{3,2,1,0:T(8,128)(2,1)S(1)}, bf16[16,4,6,1]{3,2,1,0:T(8,128)(2,1)S(1)}, u32[]{:S(2)}, u32[]{:S(2)}) collective-permute-start(bf16[16,4,6,1]{3,2,1,0:T(8,128)(2,1)S(1)} %get-tuple-element.15), channel_id=1, source_target_pairs={{0,1},{1,2},{2,3},{4,5},{5,6},{6,7},{8,9},{9,10},{10,11},{12,13},{... | collective-permute-start | bytes 2312 | tf_op jit(solution)/shard_map/ppermute | solution.py:19
  41.0 1.3 collective-permute-start.5
  42.4 1.1 collective-permute-done.4
  43.5 4.4 %collective-permute-done.5 = bf16[16,4,6,1]{3,2,1,0:T(8,128)(2,1)S(1)} collective-permute-done((bf16[16,4,6,1]{3,2,1,0:T(8,128)(2,1)S(1)}, bf16[16,4,6,1]{3,2,1,0:T(8,128)(2,1)S(1)}, u32[]{:S(2)}, u32[]{:S(2)}) %collective-permute-start.5) | collective-permute-done | bytes 800 | tf_op jit(solution)/shard_map/ppermute | solution.py:21
  47.8 0.9 pad_maximum_fusion
  49.3 1.6 copy.46
  55.7 0.8 copy-done
  57.3 43.2 %all-reduce = (f32[16,16]{0,1:T(8,128)S(1)}, f32[16,16]{0,1:T(8,128)S(1)}, f32[16,16]{1,0:T(8,128)S(1)}, f32[16,16]{1,0:T(8,128)S(1)}) all-reduce(f32[16,16]{0,1:T(8,128)S(1)} %convolution_bitcast_fusion.4, f32[16,16]{0,1:T(8,128)S(1)} %bitcast.265, ...), channel_id=1, replica_groups=mesh['gx'=2,'gy'=4,'gz'=4] {'gx','gy','gz'}, use_global_device_ids=true, to_apply=%region_4.0 | all-reduce | flops 1024 | bytes 8192 | tf_op jit(solution)/shard_map/psum | solution.py:102
  100.6 1.5 cholesky.70
  102.1 0.6 compare_reduce_fusion.1
  102.8 0.6 fusion.56
  103.4 1.2 custom-call.10
  104.7 1.5 cholesky.59
  106.2 0.6 compare_reduce_fusion.2
  106.9 0.6 fusion.55
  107.5 1.2 custom-call.9
  110.8 4.2 %collective-permute-start.12 = (bf16[16,1,4,256]{3,0,2,1:T(8,128)(2,1)S(1)}, bf16[16,1,4,256]{3,0,2,1:T(8,128)(2,1)S(1)}, u32[]{:S(2)}, u32[]{:S(2)}) collective-permute-start(bf16[16,1,4,256]{3,0,2,1:T(8,128)(2,1)S(1)} %get-tuple-element.24), channel_id=1, source_target_pairs={{0,16},{1,17},{2,18},{3,19},{4,20},{5,21},{6,22},{7,23},{8,24},{9,... | collective-permute-start | bytes 98312 | tf_op jit(solution)/shard_map/ppermute | solution.py:19
  115.0 1.3 collective-permute-start.13
  116.6 4.2 %collective-permute-done.13 = bf16[16,1,4,256]{3,0,2,1:T(8,128)(2,1)S(1)} collective-permute-done((bf16[16,1,4,256]{3,0,2,1:T(8,128)(2,1)S(1)}, bf16[16,1,4,256]{3,0,2,1:T(8,128)(2,1)S(1)}, u32[]{:S(2)}, u32[]{:S(2)}) %collective-permute-start.13) | collective-permute-done | bytes 32800 | tf_op jit(solution)/shard_map/ppermute | solution.py:21
  120.8 1.3 collective-permute-start.14
  122.1 1.3 collective-permute-start.15
  123.5 2.1 %collective-permute-done.15 = bf16[16,4,1,256]{3,0,2,1:T(8,128)(2,1)S(1)} collective-permute-done((bf16[16,4,1,256]{3,0,2,1:T(8,128)(2,1)S(1)}, bf16[16,4,1,256]{3,0,2,1:T(8,128)(2,1)S(1)}, u32[]{:S(2)}, u32[]{:S(2)}) %collective-permute-start.15) | collective-permute-done | bytes 32800 | tf_op jit(solution)/shard_map/ppermute | solution.py:21
  125.7 2.3 %collective-permute-start.16 = (bf16[16,4,6,1]{3,0,2,1:T(8,128)(2,1)S(1)}, bf16[16,4,6,1]{3,0,2,1:T(8,128)(2,1)S(1)}, u32[]{:S(2)}, u32[]{:S(2)}) collective-permute-start(bf16[16,4,6,1]{3,0,2,1:T(8,128)(2,1)S(1)} %get-tuple-element.19), channel_id=1, source_target_pairs={{0,1},{1,2},{2,3},{4,5},{5,6},{6,7},{8,9},{9,10},{10,11},{12,13},{... | collective-permute-start | bytes 2312 | tf_op jit(solution)/shard_map/ppermute | solution.py:19
  128.1 1.3 collective-permute-start.17
  130.3 4.3 %collective-permute-done.17 = bf16[16,4,6,1]{3,0,2,1:T(8,128)(2,1)S(1)} collective-permute-done((bf16[16,4,6,1]{3,0,2,1:T(8,128)(2,1)S(1)}, bf16[16,4,6,1]{3,0,2,1:T(8,128)(2,1)S(1)}, u32[]{:S(2)}, u32[]{:S(2)}) %collective-permute-start.17) | collective-permute-done | bytes 800 | tf_op jit(solution)/shard_map/ppermute | solution.py:21
  140.0 39.1 %psum.39 = f32[16,16]{0,1:T(8,128)S(1)} all-reduce(f32[16,16]{0,1:T(8,128)S(1)} %convolution_bitcast_fusion.1), channel_id=1, replica_groups=mesh['gx'=2,'gy'=4,'gz'=4] {'gx','gy','gz'}, use_global_device_ids=true, to_apply=%region_7.10 | all-reduce | flops 256 | bytes 2048 | tf_op jit(solution)/shard_map/psum | solution.py:127
  179.3 1.5 cholesky.81
  180.7 0.6 compare_reduce_fusion
  181.4 0.6 fusion.57
  182.0 1.2 custom-call.11
  184.0 0.7 copy.45
  185.0 0.7 copy.44
  (117 shorter events, 16.9 us)
Async XLA Ops:
  1.4 13.0 %collective-permute-start.6 = (f32[1,4,256]{2,1,0:T(4,128)S(1)}, f32[1,4,256]{2,1,0:T(4,128)S(1)}, u32[]{:S(2)}, u32[]{:S(2)}) collective-permute-start(f32[1,4,256]{2,1,0:T(4,128)S(1)} %get-tuple-element.42), channel_id=1, source_target_pairs={{0,16},{1,17},{2,18},{3,19},{4,20},{5,21},{6,22},{7,23},{8,24},{9,... | collective-permute-start | bytes 12296 | tf_op jit(solution)/shard_map/ppermute | solution.py:19
  6.4 8.1 %collective-permute-start.7 = (f32[1,4,256]{2,1,0:T(4,128)S(1)}, f32[1,4,256]{2,1,0:T(4,128)S(1)}, u32[]{:S(2)}, u32[]{:S(2)}) collective-permute-start(f32[1,4,256]{2,1,0:T(4,128)S(1)} %get-tuple-element.43), channel_id=1, source_target_pairs={{16,0},{17,1},{18,2},{19,3},{20,4},{21,5},{22,6},{23,7},{24,8},{25... | collective-permute-start | bytes 12296 | tf_op jit(solution)/shard_map/ppermute | solution.py:21
  8.6 21.3 %collective-permute-start = (bf16[16,1,4,256]{3,2,1,0:T(4,128)(2,1)S(1)}, bf16[16,1,4,256]{3,2,1,0:T(4,128)(2,1)S(1)}, u32[]{:S(2)}, u32[]{:S(2)}) collective-permute-start(bf16[16,1,4,256]{3,2,1,0:T(4,128)(2,1)S(1)} %get-tuple-element.26), channel_id=1, source_target_pairs={{0,16},{1,17},{2,18},{3,19},{4,20},{5,21},{6,22},{7,23},{8,24},{9,... | collective-permute-start | bytes 98312 | tf_op jit(solution)/shard_map/ppermute | solution.py:19
  13.2 16.8 %collective-permute-start.1 = (bf16[16,1,4,256]{3,2,1,0:T(4,128)(2,1)S(1)}, bf16[16,1,4,256]{3,2,1,0:T(4,128)(2,1)S(1)}, u32[]{:S(2)}, u32[]{:S(2)}) collective-permute-start(bf16[16,1,4,256]{3,2,1,0:T(4,128)(2,1)S(1)} %get-tuple-element.27), channel_id=1, source_target_pairs={{16,0},{17,1},{18,2},{19,3},{20,4},{21,5},{22,6},{23,7},{24,8},{25... | collective-permute-start | bytes 98312 | tf_op jit(solution)/shard_map/ppermute | solution.py:21
  14.5 3.9 %collective-permute-start.8 = (f32[4,1,256]{2,1,0:T(1,128)S(1)}, f32[4,1,256]{2,1,0:T(1,128)S(1)}, u32[]{:S(2)}, u32[]{:S(2)}) collective-permute-start(f32[4,1,256]{2,1,0:T(1,128)S(1)} %get-tuple-element.40), channel_id=1, source_target_pairs={{0,4},{4,8},{8,12},{1,5},{5,9},{9,13},{2,6},{6,10},{10,14},{3,7},{... | collective-permute-start | bytes 12296 | tf_op jit(solution)/shard_map/ppermute | solution.py:19
  15.8 4.8 %collective-permute-start.9 = (f32[4,1,256]{2,1,0:T(1,128)S(1)}, f32[4,1,256]{2,1,0:T(1,128)S(1)}, u32[]{:S(2)}, u32[]{:S(2)}) collective-permute-start(f32[4,1,256]{2,1,0:T(1,128)S(1)} %get-tuple-element.41), channel_id=1, source_target_pairs={{4,0},{8,4},{12,8},{5,1},{9,5},{13,9},{6,2},{10,6},{14,10},{7,3},{... | collective-permute-start | bytes 12296 | tf_op jit(solution)/shard_map/ppermute | solution.py:21
  20.7 4.9 %collective-permute-start.10 = (f32[4,6,1]{2,1,0:T(8,128)S(1)}, f32[4,6,1]{2,1,0:T(8,128)S(1)}, u32[]{:S(2)}, u32[]{:S(2)}) collective-permute-start(f32[4,6,1]{2,1,0:T(8,128)S(1)} %get-tuple-element.36), channel_id=1, source_target_pairs={{0,1},{1,2},{2,3},{4,5},{5,6},{6,7},{8,9},{9,10},{10,11},{12,13},{... | collective-permute-start | bytes 296 | tf_op jit(solution)/shard_map/ppermute | solution.py:19
  24.2 5.6 %collective-permute-start.11 = (f32[4,6,1]{2,1,0:T(8,128)S(1)}, f32[4,6,1]{2,1,0:T(8,128)S(1)}, u32[]{:S(2)}, u32[]{:S(2)}) collective-permute-start(f32[4,6,1]{2,1,0:T(8,128)S(1)} %get-tuple-element.37), channel_id=1, source_target_pairs={{1,0},{2,1},{3,2},{5,4},{6,5},{7,6},{9,8},{10,9},{11,10},{13,12},{... | collective-permute-start | bytes 296 | tf_op jit(solution)/shard_map/ppermute | solution.py:21
  30.1 4.2 %collective-permute-start.2 = (bf16[16,4,1,256]{3,2,1,0:T(2,128)(2,1)S(1)}, bf16[16,4,1,256]{3,2,1,0:T(2,128)(2,1)S(1)}, u32[]{:S(2)}, u32[]{:S(2)}) collective-permute-start(bf16[16,4,1,256]{3,2,1,0:T(2,128)(2,1)S(1)} %get-tuple-element.22), channel_id=1, source_target_pairs={{0,4},{4,8},{8,12},{1,5},{5,9},{9,13},{2,6},{6,10},{10,14},{3,7},{... | collective-permute-start | bytes 98312 | tf_op jit(solution)/shard_map/ppermute | solution.py:19
  33.0 4.2 %collective-permute-start.3 = (bf16[16,4,1,256]{3,2,1,0:T(2,128)(2,1)S(1)}, bf16[16,4,1,256]{3,2,1,0:T(2,128)(2,1)S(1)}, u32[]{:S(2)}, u32[]{:S(2)}) collective-permute-start(bf16[16,4,1,256]{3,2,1,0:T(2,128)(2,1)S(1)} %get-tuple-element.23), channel_id=1, source_target_pairs={{4,0},{8,4},{12,8},{5,1},{9,5},{13,9},{6,2},{10,6},{14,10},{7,3},{... | collective-permute-start | bytes 98312 | tf_op jit(solution)/shard_map/ppermute | solution.py:21
  37.5 6.0 %collective-permute-start.4 = (bf16[16,4,6,1]{3,2,1,0:T(8,128)(2,1)S(1)}, bf16[16,4,6,1]{3,2,1,0:T(8,128)(2,1)S(1)}, u32[]{:S(2)}, u32[]{:S(2)}) collective-permute-start(bf16[16,4,6,1]{3,2,1,0:T(8,128)(2,1)S(1)} %get-tuple-element.15), channel_id=1, source_target_pairs={{0,1},{1,2},{2,3},{4,5},{5,6},{6,7},{8,9},{9,10},{10,11},{12,13},{... | collective-permute-start | bytes 2312 | tf_op jit(solution)/shard_map/ppermute | solution.py:19
  41.0 6.9 %collective-permute-start.5 = (bf16[16,4,6,1]{3,2,1,0:T(8,128)(2,1)S(1)}, bf16[16,4,6,1]{3,2,1,0:T(8,128)(2,1)S(1)}, u32[]{:S(2)}, u32[]{:S(2)}) collective-permute-start(bf16[16,4,6,1]{3,2,1,0:T(8,128)(2,1)S(1)} %get-tuple-element.14), channel_id=1, source_target_pairs={{1,0},{2,1},{3,2},{5,4},{6,5},{7,6},{9,8},{10,9},{11,10},{13,12},{... | collective-permute-start | bytes 2312 | tf_op jit(solution)/shard_map/ppermute | solution.py:21
  49.3 1.6 copy-start.1
  51.0 0.7 copy-start.2
  51.0 1.2 copy-start.3
  51.6 1.1 copy-start.4
  52.2 1.1 copy-start.5
  52.7 1.1 copy-start.6
  53.3 1.1 copy-start.7
  53.8 1.1 copy-start.8
  55.6 0.9 copy-start
  110.8 5.8 %collective-permute-start.12 = (bf16[16,1,4,256]{3,0,2,1:T(8,128)(2,1)S(1)}, bf16[16,1,4,256]{3,0,2,1:T(8,128)(2,1)S(1)}, u32[]{:S(2)}, u32[]{:S(2)}) collective-permute-start(bf16[16,1,4,256]{3,0,2,1:T(8,128)(2,1)S(1)} %get-tuple-element.24), channel_id=1, source_target_pairs={{0,16},{1,17},{2,18},{3,19},{4,20},{5,21},{6,22},{7,23},{8,24},{9,... | collective-permute-start | bytes 98312 | tf_op jit(solution)/shard_map/ppermute | solution.py:19
  115.0 5.8 %collective-permute-start.13 = (bf16[16,1,4,256]{3,0,2,1:T(8,128)(2,1)S(1)}, bf16[16,1,4,256]{3,0,2,1:T(8,128)(2,1)S(1)}, u32[]{:S(2)}, u32[]{:S(2)}) collective-permute-start(bf16[16,1,4,256]{3,0,2,1:T(8,128)(2,1)S(1)} %get-tuple-element.25), channel_id=1, source_target_pairs={{16,0},{17,1},{18,2},{19,3},{20,4},{21,5},{22,6},{23,7},{24,8},{25... | collective-permute-start | bytes 98312 | tf_op jit(solution)/shard_map/ppermute | solution.py:21
  120.8 2.6 %collective-permute-start.14 = (bf16[16,4,1,256]{3,0,2,1:T(8,128)(2,1)S(1)}, bf16[16,4,1,256]{3,0,2,1:T(8,128)(2,1)S(1)}, u32[]{:S(2)}, u32[]{:S(2)}) collective-permute-start(bf16[16,4,1,256]{3,0,2,1:T(8,128)(2,1)S(1)} %get-tuple-element.20), channel_id=1, source_target_pairs={{0,4},{4,8},{8,12},{1,5},{5,9},{9,13},{2,6},{6,10},{10,14},{3,7},{... | collective-permute-start | bytes 98312 | tf_op jit(solution)/shard_map/ppermute | solution.py:19
  122.1 3.5 %collective-permute-start.15 = (bf16[16,4,1,256]{3,0,2,1:T(8,128)(2,1)S(1)}, bf16[16,4,1,256]{3,0,2,1:T(8,128)(2,1)S(1)}, u32[]{:S(2)}, u32[]{:S(2)}) collective-permute-start(bf16[16,4,1,256]{3,0,2,1:T(8,128)(2,1)S(1)} %get-tuple-element.21), channel_id=1, source_target_pairs={{4,0},{8,4},{12,8},{5,1},{9,5},{13,9},{6,2},{10,6},{14,10},{7,3},{... | collective-permute-start | bytes 98312 | tf_op jit(solution)/shard_map/ppermute | solution.py:21
  125.7 4.5 %collective-permute-start.16 = (bf16[16,4,6,1]{3,0,2,1:T(8,128)(2,1)S(1)}, bf16[16,4,6,1]{3,0,2,1:T(8,128)(2,1)S(1)}, u32[]{:S(2)}, u32[]{:S(2)}) collective-permute-start(bf16[16,4,6,1]{3,0,2,1:T(8,128)(2,1)S(1)} %get-tuple-element.19), channel_id=1, source_target_pairs={{0,1},{1,2},{2,3},{4,5},{5,6},{6,7},{8,9},{9,10},{10,11},{12,13},{... | collective-permute-start | bytes 2312 | tf_op jit(solution)/shard_map/ppermute | solution.py:19
  128.1 6.5 %collective-permute-start.17 = (bf16[16,4,6,1]{3,0,2,1:T(8,128)(2,1)S(1)}, bf16[16,4,6,1]{3,0,2,1:T(8,128)(2,1)S(1)}, u32[]{:S(2)}, u32[]{:S(2)}) collective-permute-start(bf16[16,4,6,1]{3,0,2,1:T(8,128)(2,1)S(1)} %get-tuple-element.18), channel_id=1, source_target_pairs={{1,0},{2,1},{3,2},{5,4},{6,5},{7,6},{9,8},{10,9},{11,10},{13,12},{... | collective-permute-start | bytes 2312 | tf_op jit(solution)/shard_map/ppermute | solution.py:21
where the time goes:
time: 187 us; the launch traced here: 186 us
  blocking collectives  82.4 us (44%)
  starting transfers between devices  40 us (21%)
  waiting for transfers between devices  26.4 us (14%)
  other arithmetic  15.8 us (8%)
  matrix products  13.6 us (7%)
  local copies, waits for them, and re-layouts  6.08 us (3%)
    psum x1, blocking collectives, residual_gram(): return lax.psum(local_gram(residual, residual), ('gx', 'gy', 'gz'))  43.2 us
    psum x1, blocking collectives, on_device(): lax.psum((local_gram(direction, image), local_gram(image, residual), loca...  39.1 us
    ppermute x9, starting transfers between devices, padded_2(): lax.ppermute(tail, axis, [(i, (i + 1) % count) for i in range(ends)])  28.4 us
    ppermute x9, waiting for transfers between devices, padded_2(): lax.ppermute(head, axis, [((i + 1) % count, i) for i in range(ends)])  24.2 us
    ppermute x9, starting transfers between devices, padded_2(): lax.ppermute(head, axis, [((i + 1) % count, i) for i in range(ends)])  11.6 us
    dot_general x16, matrix products, apply_operator(): jnp.einsum('b,bcxyz->cxyz', kernel[corner], stacked, preferred_element_ty...  8.36 us
    another operation x9, other arithmetic, solve_small(): factor = jnp.linalg.cholesky(matrix)  6.4 us
    another operation x6, other arithmetic, solve_small(): return jax.scipy.linalg.cho_solve((factor, True), rhs_small)  5.63 us
  transfers between devices with their start and end apart: 18, of which 12 were waited for; matrix products, arithmetic and copies ran while one was open for 2% of the time, Pallas kernels for 0%

commit v1 on v0

--- a/solution.py
+++ b/solution.py
@@ -125,8 +125,15 @@
     for iteration in range(ITERS):
         image = apply_operator(direction, weights, kernel)
         curvature, cross, image_sq = lax.psum(
-            (local_gram(direction, image), local_gram(image, residual), local_gram(image, image)),
-            ("gx", "gy", "gz"),
+            lax.psum(
+                (
+                    local_gram(direction, image),
+                    local_gram(image, residual),
+                    local_gram(image, image),
+                ),
+                "gx",
+            ),
+            ("gy", "gz"),
         )
         alpha = solve_small(curvature, current)
         solution = solution + combine(direction, alpha)

time: 187 us -> 249 us (1.33)
  blocking collectives: 82.4 us -> 143 us
  waiting for transfers between devices: 26.4 us -> 29.9 us
    psum x0 -> x2, blocking collectives: none -> 88.9 us  [on_device(): lax.psum(lax.psum((local_gram(direction, image), local_gram(image, residu...]
    psum x1 -> x2, blocking collectives: 39.1 us -> 12.4 us  [on_device(): lax.psum((local_gram(direction, image), local_gram(image, residual), loca...]
    ppermute x9, waiting for transfers between devices: 24.2 us -> 27.8 us  [padded_2(): lax.ppermute(head, axis, [((i + 1) % count, i) for i in range(ends)])]
  transfers between devices with their start and end apart: 18 -> 18, of which waited for: 12 -> 11; matrix products, arithmetic and copies ran while one was open for 2% -> 3% of each run, Pallas kernels for 0% -> 0%
where the time goes in v1:
time: 249 us; the launch traced here: 248 us
  blocking collectives  143 us (57%)
  starting transfers between devices  38.5 us (15%)
  waiting for transfers between devices  29.9 us (12%)
  other arithmetic  15.8 us (6%)
  matrix products  13.6 us (5%)
  local copies, waits for them, and re-layouts  6.08 us (2%)
    psum x2, blocking collectives, on_device(): lax.psum(lax.psum((local_gram(direction, image), local_gram(image, residu...  88.9 us
    psum x1, blocking collectives, residual_gram(): return lax.psum(local_gram(residual, residual), ('gx', 'gy', 'gz'))  41.7 us
    ppermute x9, waiting for transfers between devices, padded_2(): lax.ppermute(head, axis, [((i + 1) % count, i) for i in range(ends)])  27.8 us
    ppermute x9, starting transfers between devices, padded_2(): lax.ppermute(tail, axis, [(i, (i + 1) % count) for i in range(ends)])  26.9 us
    psum x2, blocking collectives, on_device(): lax.psum((local_gram(direction, image), local_gram(image, residual), loca...  12.4 us
    ppermute x9, starting transfers between devices, padded_2(): lax.ppermute(head, axis, [((i + 1) % count, i) for i in range(ends)])  11.6 us
    dot_general x16, matrix products, apply_operator(): jnp.einsum('b,bcxyz->cxyz', kernel[corner], stacked, preferred_element_ty...  8.39 us
    another operation x9, other arithmetic, solve_small(): factor = jnp.linalg.cholesky(matrix)  6.39 us
  transfers between devices with their start and end apart: 18, of which 11 were waited for; matrix products, arithmetic and copies ran while one was open for 3% of the time, Pallas kernels for 0%

profile of v1, /device:TPU:0, one launch (start us, length us, event | category | flops | bytes accessed | tf_op | source)
XLA Modules:
  0.0 248.3 jit_solution(6272701478678985922)
XLA Ops:
  0.6 0.9 convert_element_type.9
  1.6 4.9 %collective-permute-start = (bf16[16,1,4,256]{3,2,1,0:T(4,128)(2,1)S(1)}, bf16[16,1,4,256]{3,2,1,0:T(4,128)(2,1)S(1)}, u32[]{:S(2)}, u32[]{:S(2)}) collective-permute-start(bf16[16,1,4,256]{3,2,1,0:T(4,128)(2,1)S(1)} %get-tuple-element.28), channel_id=1, source_target_pairs={{0,16},{1,17},{2,18},{3,19},{4,20},{5,21},{6,22},{7,23},{8,24},{9,... | collective-permute-start | bytes 98312 | tf_op jit(solution)/shard_map/ppermute | solution.py:19
  6.5 1.3 collective-permute-start.1
  7.8 0.8 select_reduce_fusion
  8.6 4.5 %collective-permute-start.6 = (f32[1,4,256]{2,1,0:T(4,128)S(1)}, f32[1,4,256]{2,1,0:T(4,128)S(1)}, u32[]{:S(2)}, u32[]{:S(2)}) collective-permute-start(f32[1,4,256]{2,1,0:T(4,128)S(1)} %get-tuple-element.44), channel_id=1, source_target_pairs={{0,16},{1,17},{2,18},{3,19},{4,20},{5,21},{6,22},{7,23},{8,24},{9,... | collective-permute-start | bytes 12296 | tf_op jit(solution)/shard_map/ppermute | solution.py:19
  13.2 1.3 collective-permute-start.7
  14.5 1.3 convolution_bitcast_fusion.4
  15.7 41.7 %psum.65 = f32[16,16]{0,1:T(8,128)S(1)} all-reduce(f32[16,16]{0,1:T(8,128)S(1)} %convolution_bitcast_fusion.4), channel_id=1, replica_groups=mesh['gx'=2,'gy'=4,'gz'=4] {'gx','gy','gz'}, use_global_device_ids=true, to_apply=%region_5.0 | all-reduce | flops 256 | bytes 2048 | tf_op jit(solution)/shard_map/psum | solution.py:102
  57.5 1.5 cholesky.70
  59.7 1.3 collective-permute-start.8
  60.9 1.3 collective-permute-start.9
  62.2 0.7 fusion.56
  62.9 1.2 custom-call.10
  64.1 2.4 collective-permute-done.9
  66.6 3.4 %collective-permute-start.10 = (f32[4,6,1]{2,1,0:T(8,128)S(1)}, f32[4,6,1]{2,1,0:T(8,128)S(1)}, u32[]{:S(2)}, u32[]{:S(2)}) collective-permute-start(f32[4,6,1]{2,1,0:T(8,128)S(1)} %get-tuple-element.38), channel_id=1, source_target_pairs={{0,1},{1,2},{2,3},{4,5},{5,6},{6,7},{8,9},{9,10},{10,11},{12,13},{... | collective-permute-start | bytes 296 | tf_op jit(solution)/shard_map/ppermute | solution.py:19
  70.0 1.3 collective-permute-start.11
  71.4 4.2 %collective-permute-done.11 = f32[4,6,1]{2,1,0:T(8,128)S(1)} collective-permute-done((f32[4,6,1]{2,1,0:T(8,128)S(1)}, f32[4,6,1]{2,1,0:T(8,128)S(1)}, u32[]{:S(2)}, u32[]{:S(2)}) %collective-permute-start.11) | collective-permute-done | bytes 128 | tf_op jit(solution)/shard_map/ppermute | solution.py:21
  76.0 2.8 %collective-permute-start.2 = (bf16[16,4,1,256]{3,2,1,0:T(2,128)(2,1)S(1)}, bf16[16,4,1,256]{3,2,1,0:T(2,128)(2,1)S(1)}, u32[]{:S(2)}, u32[]{:S(2)}) collective-permute-start(bf16[16,4,1,256]{3,2,1,0:T(2,128)(2,1)S(1)} %get-tuple-element.24), channel_id=1, source_target_pairs={{0,4},{4,8},{8,12},{1,5},{5,9},{9,13},{2,6},{6,10},{10,14},{3,7},{... | collective-permute-start | bytes 98312 | tf_op jit(solution)/shard_map/ppermute | solution.py:19
  78.8 1.3 collective-permute-start.3
  80.2 3.4 %collective-permute-done.3 = bf16[16,4,1,256]{3,2,1,0:T(2,128)(2,1)S(1)} collective-permute-done((bf16[16,4,1,256]{3,2,1,0:T(2,128)(2,1)S(1)}, bf16[16,4,1,256]{3,2,1,0:T(2,128)(2,1)S(1)}, u32[]{:S(2)}, u32[]{:S(2)}) %collective-permute-start.3) | collective-permute-done | bytes 32800 | tf_op jit(solution)/shard_map/ppermute | solution.py:21
  83.9 3.3 %collective-permute-start.4 = (bf16[16,4,6,1]{3,2,1,0:T(8,128)(2,1)S(1)}, bf16[16,4,6,1]{3,2,1,0:T(8,128)(2,1)S(1)}, u32[]{:S(2)}, u32[]{:S(2)}) collective-permute-start(bf16[16,4,6,1]{3,2,1,0:T(8,128)(2,1)S(1)} %get-tuple-element.17), channel_id=1, source_target_pairs={{0,1},{1,2},{2,3},{4,5},{5,6},{6,7},{8,9},{9,10},{10,11},{12,13},{... | collective-permute-start | bytes 2312 | tf_op jit(solution)/shard_map/ppermute | solution.py:19
  87.2 1.3 collective-permute-start.5
  88.6 1.1 collective-permute-done.4
  89.7 4.4 %collective-permute-done.5 = bf16[16,4,6,1]{3,2,1,0:T(8,128)(2,1)S(1)} collective-permute-done((bf16[16,4,6,1]{3,2,1,0:T(8,128)(2,1)S(1)}, bf16[16,4,6,1]{3,2,1,0:T(8,128)(2,1)S(1)}, u32[]{:S(2)}, u32[]{:S(2)}) %collective-permute-start.5) | collective-permute-done | bytes 800 | tf_op jit(solution)/shard_map/ppermute | solution.py:21
  94.1 0.9 pad_maximum_fusion
  95.5 1.6 copy.46
  102.0 0.8 copy-done
  103.5 7.4 %all-reduce.1 = (f32[16,16]{0,1:T(8,128)S(1)}, f32[16,16]{1,0:T(8,128)S(1)}, f32[16,16]{1,0:T(8,128)S(1)}) all-reduce(f32[16,16]{0,1:T(8,128)S(1)} %bitcast.265, f32[16,16]{1,0:T(8,128)S(1)} %convolution_bitcast_fusion.3, f32[16,16]{1,0:T(8,128)S(1)} %bitcast.266), channel_id=1, replica_groups=mesh['gx'=2,'gy'=4,'gz'=4] {'gx'}, use_global_device_ids=true, to_apply=%region_1.2 | all-reduce | flops 768 | bytes 6144 | tf_op jit(solution)/shard_map/psum | solution.py:128
  110.9 58.2 %all-reduce = (f32[16,16]{0,1:T(8,128)S(1)}, f32[16,16]{1,0:T(8,128)S(1)}, f32[16,16]{1,0:T(8,128)S(1)}) all-reduce(f32[16,16]{0,1:T(8,128)S(1)} %get-tuple-element.11, f32[16,16]{1,0:T(8,128)S(1)} %get-tuple-element.12, f32[16,16]{1,0:T(8,128)S(1)} %get-tuple-element.13), channel_id=1, replica_groups=mesh['gx'=2,'gy'=4,'gz'=4] {'gy','gz'}, use_global_device_ids=true, to_apply=%region_2.3 | all-reduce | flops 768 | bytes 6144 | tf_op jit(solution)/shard_map/psum | solution.py:127
  169.2 1.5 cholesky.59
  171.4 0.6 fusion.55
  172.0 1.2 custom-call.9
  175.3 3.4 %collective-permute-start.12 = (bf16[16,1,4,256]{3,0,2,1:T(8,128)(2,1)S(1)}, bf16[16,1,4,256]{3,0,2,1:T(8,128)(2,1)S(1)}, u32[]{:S(2)}, u32[]{:S(2)}) collective-permute-start(bf16[16,1,4,256]{3,0,2,1:T(8,128)(2,1)S(1)} %get-tuple-element.26), channel_id=1, source_target_pairs={{0,16},{1,17},{2,18},{3,19},{4,20},{5,21},{6,22},{7,23},{8,24},{9,... | collective-permute-start | bytes 98312 | tf_op jit(solution)/shard_map/ppermute | solution.py:19
  178.7 1.3 collective-permute-start.13
  180.3 4.2 %collective-permute-done.13 = bf16[16,1,4,256]{3,0,2,1:T(8,128)(2,1)S(1)} collective-permute-done((bf16[16,1,4,256]{3,0,2,1:T(8,128)(2,1)S(1)}, bf16[16,1,4,256]{3,0,2,1:T(8,128)(2,1)S(1)}, u32[]{:S(2)}, u32[]{:S(2)}) %collective-permute-start.13) | collective-permute-done | bytes 32800 | tf_op jit(solution)/shard_map/ppermute | solution.py:21
  184.5 1.3 collective-permute-start.14
  185.8 1.3 collective-permute-start.15
  187.2 4.9 %collective-permute-done.15 = bf16[16,4,1,256]{3,0,2,1:T(8,128)(2,1)S(1)} collective-permute-done((bf16[16,4,1,256]{3,0,2,1:T(8,128)(2,1)S(1)}, bf16[16,4,1,256]{3,0,2,1:T(8,128)(2,1)S(1)}, u32[]{:S(2)}, u32[]{:S(2)}) %collective-permute-start.15) | collective-permute-done | bytes 32800 | tf_op jit(solution)/shard_map/ppermute | solution.py:21
  192.2 1.9 collective-permute-start.16
  194.1 1.3 collective-permute-start.17
  196.3 4.3 %collective-permute-done.17 = bf16[16,4,6,1]{3,0,2,1:T(8,128)(2,1)S(1)} collective-permute-done((bf16[16,4,6,1]{3,0,2,1:T(8,128)(2,1)S(1)}, bf16[16,4,6,1]{3,0,2,1:T(8,128)(2,1)S(1)}, u32[]{:S(2)}, u32[]{:S(2)}) %collective-permute-start.17) | collective-permute-done | bytes 800 | tf_op jit(solution)/shard_map/ppermute | solution.py:21
  206.1 5.0 %psum.70 = f32[16,16]{0,1:T(8,128)S(1)} all-reduce(f32[16,16]{0,1:T(8,128)S(1)} %convolution_bitcast_fusion.1), channel_id=1, replica_groups=mesh['gx'=2,'gy'=4,'gz'=4] {'gx'}, use_global_device_ids=true, to_apply=%region_10.13 | all-reduce | flops 256 | bytes 2048 | tf_op jit(solution)/shard_map/psum | solution.py:128
  211.1 30.6 %psum.71 = f32[16,16]{0,1:T(8,128)S(1)} all-reduce(f32[16,16]{0,1:T(8,128)S(1)} %psum.70), channel_id=1, replica_groups=mesh['gx'=2,'gy'=4,'gz'=4] {'gy','gz'}, use_global_device_ids=true, to_apply=%region_11.14 | all-reduce | flops 256 | bytes 2048 | tf_op jit(solution)/shard_map/psum | solution.py:127
  241.8 1.5 cholesky.81
  244.0 0.6 fusion.57
  244.6 1.2 custom-call.11
  246.5 0.7 copy.45
  247.5 0.7 copy.44
  (120 shorter events, 18.8 us)
Async XLA Ops:
  1.6 74.2 %collective-permute-start = (bf16[16,1,4,256]{3,2,1,0:T(4,128)(2,1)S(1)}, bf16[16,1,4,256]{3,2,1,0:T(4,128)(2,1)S(1)}, u32[]{:S(2)}, u32[]{:S(2)}) collective-permute-start(bf16[16,1,4,256]{3,2,1,0:T(4,128)(2,1)S(1)} %get-tuple-element.28), channel_id=1, source_target_pairs={{0,16},{1,17},{2,18},{3,19},{4,20},{5,21},{6,22},{7,23},{8,24},{9,... | collective-permute-start | bytes 98312 | tf_op jit(solution)/shard_map/ppermute | solution.py:19
  6.5 69.3 %collective-permute-start.1 = (bf16[16,1,4,256]{3,2,1,0:T(4,128)(2,1)S(1)}, bf16[16,1,4,256]{3,2,1,0:T(4,128)(2,1)S(1)}, u32[]{:S(2)}, u32[]{:S(2)}) collective-permute-start(bf16[16,1,4,256]{3,2,1,0:T(4,128)(2,1)S(1)} %get-tuple-element.29), channel_id=1, source_target_pairs={{16,0},{17,1},{18,2},{19,3},{20,4},{21,5},{22,6},{23,7},{24,8},{25... | collective-permute-start | bytes 98312 | tf_op jit(solution)/shard_map/ppermute | solution.py:21
  8.6 51.0 %collective-permute-start.6 = (f32[1,4,256]{2,1,0:T(4,128)S(1)}, f32[1,4,256]{2,1,0:T(4,128)S(1)}, u32[]{:S(2)}, u32[]{:S(2)}) collective-permute-start(f32[1,4,256]{2,1,0:T(4,128)S(1)} %get-tuple-element.44), channel_id=1, source_target_pairs={{0,16},{1,17},{2,18},{3,19},{4,20},{5,21},{6,22},{7,23},{8,24},{9,... | collective-permute-start | bytes 12296 | tf_op jit(solution)/shard_map/ppermute | solution.py:19
  13.2 46.5 %collective-permute-start.7 = (f32[1,4,256]{2,1,0:T(4,128)S(1)}, f32[1,4,256]{2,1,0:T(4,128)S(1)}, u32[]{:S(2)}, u32[]{:S(2)}) collective-permute-start(f32[1,4,256]{2,1,0:T(4,128)S(1)} %get-tuple-element.45), channel_id=1, source_target_pairs={{16,0},{17,1},{18,2},{19,3},{20,4},{21,5},{22,6},{23,7},{24,8},{25... | collective-permute-start | bytes 12296 | tf_op jit(solution)/shard_map/ppermute | solution.py:21
  59.7 4.5 %collective-permute-start.8 = (f32[4,1,256]{2,1,0:T(1,128)S(1)}, f32[4,1,256]{2,1,0:T(1,128)S(1)}, u32[]{:S(2)}, u32[]{:S(2)}) collective-permute-start(f32[4,1,256]{2,1,0:T(1,128)S(1)} %get-tuple-element.42), channel_id=1, source_target_pairs={{0,4},{4,8},{8,12},{1,5},{5,9},{9,13},{2,6},{6,10},{10,14},{3,7},{... | collective-permute-start | bytes 12296 | tf_op jit(solution)/shard_map/ppermute | solution.py:19
  60.9 5.6 %collective-permute-start.9 = (f32[4,1,256]{2,1,0:T(1,128)S(1)}, f32[4,1,256]{2,1,0:T(1,128)S(1)}, u32[]{:S(2)}, u32[]{:S(2)}) collective-permute-start(f32[4,1,256]{2,1,0:T(1,128)S(1)} %get-tuple-element.43), channel_id=1, source_target_pairs={{4,0},{8,4},{12,8},{5,1},{9,5},{13,9},{6,2},{10,6},{14,10},{7,3},{... | collective-permute-start | bytes 12296 | tf_op jit(solution)/shard_map/ppermute | solution.py:21
  66.6 4.8 %collective-permute-start.10 = (f32[4,6,1]{2,1,0:T(8,128)S(1)}, f32[4,6,1]{2,1,0:T(8,128)S(1)}, u32[]{:S(2)}, u32[]{:S(2)}) collective-permute-start(f32[4,6,1]{2,1,0:T(8,128)S(1)} %get-tuple-element.38), channel_id=1, source_target_pairs={{0,1},{1,2},{2,3},{4,5},{5,6},{6,7},{8,9},{9,10},{10,11},{12,13},{... | collective-permute-start | bytes 296 | tf_op jit(solution)/shard_map/ppermute | solution.py:19
  70.0 5.6 %collective-permute-start.11 = (f32[4,6,1]{2,1,0:T(8,128)S(1)}, f32[4,6,1]{2,1,0:T(8,128)S(1)}, u32[]{:S(2)}, u32[]{:S(2)}) collective-permute-start(f32[4,6,1]{2,1,0:T(8,128)S(1)} %get-tuple-element.39), channel_id=1, source_target_pairs={{1,0},{2,1},{3,2},{5,4},{6,5},{7,6},{9,8},{10,9},{11,10},{13,12},{... | collective-permute-start | bytes 296 | tf_op jit(solution)/shard_map/ppermute | solution.py:21
  76.0 4.2 %collective-permute-start.2 = (bf16[16,4,1,256]{3,2,1,0:T(2,128)(2,1)S(1)}, bf16[16,4,1,256]{3,2,1,0:T(2,128)(2,1)S(1)}, u32[]{:S(2)}, u32[]{:S(2)}) collective-permute-start(bf16[16,4,1,256]{3,2,1,0:T(2,128)(2,1)S(1)} %get-tuple-element.24), channel_id=1, source_target_pairs={{0,4},{4,8},{8,12},{1,5},{5,9},{9,13},{2,6},{6,10},{10,14},{3,7},{... | collective-permute-start | bytes 98312 | tf_op jit(solution)/shard_map/ppermute | solution.py:19
  78.8 4.7 %collective-permute-start.3 = (bf16[16,4,1,256]{3,2,1,0:T(2,128)(2,1)S(1)}, bf16[16,4,1,256]{3,2,1,0:T(2,128)(2,1)S(1)}, u32[]{:S(2)}, u32[]{:S(2)}) collective-permute-start(bf16[16,4,1,256]{3,2,1,0:T(2,128)(2,1)S(1)} %get-tuple-element.25), channel_id=1, source_target_pairs={{4,0},{8,4},{12,8},{5,1},{9,5},{13,9},{6,2},{10,6},{14,10},{7,3},{... | collective-permute-start | bytes 98312 | tf_op jit(solution)/shard_map/ppermute | solution.py:21
  83.9 5.8 %collective-permute-start.4 = (bf16[16,4,6,1]{3,2,1,0:T(8,128)(2,1)S(1)}, bf16[16,4,6,1]{3,2,1,0:T(8,128)(2,1)S(1)}, u32[]{:S(2)}, u32[]{:S(2)}) collective-permute-start(bf16[16,4,6,1]{3,2,1,0:T(8,128)(2,1)S(1)} %get-tuple-element.17), channel_id=1, source_target_pairs={{0,1},{1,2},{2,3},{4,5},{5,6},{6,7},{8,9},{9,10},{10,11},{12,13},{... | collective-permute-start | bytes 2312 | tf_op jit(solution)/shard_map/ppermute | solution.py:19
  87.2 6.9 %collective-permute-start.5 = (bf16[16,4,6,1]{3,2,1,0:T(8,128)(2,1)S(1)}, bf16[16,4,6,1]{3,2,1,0:T(8,128)(2,1)S(1)}, u32[]{:S(2)}, u32[]{:S(2)}) collective-permute-start(bf16[16,4,6,1]{3,2,1,0:T(8,128)(2,1)S(1)} %get-tuple-element.16), channel_id=1, source_target_pairs={{1,0},{2,1},{3,2},{5,4},{6,5},{7,6},{9,8},{10,9},{11,10},{13,12},{... | collective-permute-start | bytes 2312 | tf_op jit(solution)/shard_map/ppermute | solution.py:21
  95.5 1.6 copy-start.1
  97.2 0.7 copy-start.2
  97.2 1.2 copy-start.3
  97.8 1.1 copy-start.4
  98.4 1.1 copy-start.5
  98.9 1.1 copy-start.6
  99.5 1.1 copy-start.7
  100.1 1.1 copy-start.8
  101.8 0.9 copy-start
  175.3 5.0 %collective-permute-start.12 = (bf16[16,1,4,256]{3,0,2,1:T(8,128)(2,1)S(1)}, bf16[16,1,4,256]{3,0,2,1:T(8,128)(2,1)S(1)}, u32[]{:S(2)}, u32[]{:S(2)}) collective-permute-start(bf16[16,1,4,256]{3,0,2,1:T(8,128)(2,1)S(1)} %get-tuple-element.26), channel_id=1, source_target_pairs={{0,16},{1,17},{2,18},{3,19},{4,20},{5,21},{6,22},{7,23},{8,24},{9,... | collective-permute-start | bytes 98312 | tf_op jit(solution)/shard_map/ppermute | solution.py:19
  178.7 5.8 %collective-permute-start.13 = (bf16[16,1,4,256]{3,0,2,1:T(8,128)(2,1)S(1)}, bf16[16,1,4,256]{3,0,2,1:T(8,128)(2,1)S(1)}, u32[]{:S(2)}, u32[]{:S(2)}) collective-permute-start(bf16[16,1,4,256]{3,0,2,1:T(8,128)(2,1)S(1)} %get-tuple-element.27), channel_id=1, source_target_pairs={{16,0},{17,1},{18,2},{19,3},{20,4},{21,5},{22,6},{23,7},{24,8},{25... | collective-permute-start | bytes 98312 | tf_op jit(solution)/shard_map/ppermute | solution.py:21
  184.5 2.6 %collective-permute-start.14 = (bf16[16,4,1,256]{3,0,2,1:T(8,128)(2,1)S(1)}, bf16[16,4,1,256]{3,0,2,1:T(8,128)(2,1)S(1)}, u32[]{:S(2)}, u32[]{:S(2)}) collective-permute-start(bf16[16,4,1,256]{3,0,2,1:T(8,128)(2,1)S(1)} %get-tuple-element.22), channel_id=1, source_target_pairs={{0,4},{4,8},{8,12},{1,5},{5,9},{9,13},{2,6},{6,10},{10,14},{3,7},{... | collective-permute-start | bytes 98312 | tf_op jit(solution)/shard_map/ppermute | solution.py:19
  185.8 6.2 %collective-permute-start.15 = (bf16[16,4,1,256]{3,0,2,1:T(8,128)(2,1)S(1)}, bf16[16,4,1,256]{3,0,2,1:T(8,128)(2,1)S(1)}, u32[]{:S(2)}, u32[]{:S(2)}) collective-permute-start(bf16[16,4,1,256]{3,0,2,1:T(8,128)(2,1)S(1)} %get-tuple-element.23), channel_id=1, source_target_pairs={{4,0},{8,4},{12,8},{5,1},{9,5},{13,9},{6,2},{10,6},{14,10},{7,3},{... | collective-permute-start | bytes 98312 | tf_op jit(solution)/shard_map/ppermute | solution.py:21
  192.2 4.1 %collective-permute-start.16 = (bf16[16,4,6,1]{3,0,2,1:T(8,128)(2,1)S(1)}, bf16[16,4,6,1]{3,0,2,1:T(8,128)(2,1)S(1)}, u32[]{:S(2)}, u32[]{:S(2)}) collective-permute-start(bf16[16,4,6,1]{3,0,2,1:T(8,128)(2,1)S(1)} %get-tuple-element.21), channel_id=1, source_target_pairs={{0,1},{1,2},{2,3},{4,5},{5,6},{6,7},{8,9},{9,10},{10,11},{12,13},{... | collective-permute-start | bytes 2312 | tf_op jit(solution)/shard_map/ppermute | solution.py:19
  194.1 6.5 %collective-permute-start.17 = (bf16[16,4,6,1]{3,0,2,1:T(8,128)(2,1)S(1)}, bf16[16,4,6,1]{3,0,2,1:T(8,128)(2,1)S(1)}, u32[]{:S(2)}, u32[]{:S(2)}) collective-permute-start(bf16[16,4,6,1]{3,0,2,1:T(8,128)(2,1)S(1)} %get-tuple-element.20), channel_id=1, source_target_pairs={{1,0},{2,1},{3,2},{5,4},{6,5},{7,6},{9,8},{10,9},{11,10},{13,12},{... | collective-permute-start | bytes 2312 | tf_op jit(solution)/shard_map/ppermute | solution.py:21
